TPU v7x, 32 devices: a whole 2x2x4 slice. The times are simulated.
32 devices in a mesh: node: 16 (over z, x, core), tone: 2 (over y).
Axes of the slice: x: 2, y: 2, z: 4, core: 2. Of those that a mesh axis runs over, the one named last changes fastest.
Arguments:
- voltages: float32 [32, 32, 16384], P(None, 'tone', 'node'), may hold values from -6 to 6
- source: float32 [32, 32, 16384], P(None, 'tone', 'node'), may hold values from -6 to 6
- coupling: float32 [128, 7, 128, 128], P('node'), may hold values from -0.1875 to 0.1875
- band_code: int32 [7], replicated, may hold values from 0 to 6, each once
- active: int32 [128, 7], P('node'), may hold values 0 or 1
- cap: float32 [16384], P('node'), may hold values from 0.5 to 2
- damp: float32 [32, 32], P(None, 'tone'), may hold values from 0.5 to 4
- kind: int32 [16384], P('node'), may hold values from 0 to 3
- type_params: float32 [3, 4], replicated, may hold values from 0.3 to 2
Outputs:
- new_voltages: float32 [32, 32, 16384], P(None, 'tone', 'node')
- remaining: float32 [32, 32, 16384], P(None, 'tone', 'node')
Inputs may be any that keep to these rules, and one draw needn't show every extreme that they name: band_code holds each of 0 to 6 once, so the bands reach every block offset from -3 to 3.
All inputs are finite; a program needn't handle non-finite values. No bound on the sum of `active` on one device may be relied on, other than what follows from the above.
Results may differ from a plain program's by a relative error of at most 0.0003.
Values sent between devices are 32-bit elements; how exact they have to be, the bound alone decides.
No kernel may reach another device: no remote copies, remote signals or barrier semaphores. Data moves between devices by JAX's collectives and lax.ppermute only.
A program may use at most 128 MiB of HBM per device.

v0:
```python
import math
import jax
import jax.numpy as jnp
from jax import lax
from jax.sharding import PartitionSpec as P

K1 = 32
K2 = 32
NB = 128
HALO_B = 3
NOFF = 7
M = 4
NTYPES = 4
HIGH = lax.Precision.HIGHEST


def extended(value, sides, width):
    for axis, dim in sides:
        count, length = (lax.axis_size(axis), value.shape[dim])
        up = [(i, (i + 1) % count) for i in range(count - 1)]
        down = [(j, i) for i, j in up]
        last = lax.slice_in_dim(value, length - width, length, axis=dim)
        leading = lax.slice_in_dim(value, 0, width, axis=dim)
        before = lax.ppermute(last, axis, up)
        after = lax.ppermute(leading, axis, down)
        value = jnp.concatenate([before, value, after], axis=dim)
    return value


def hartley(count):
    grid = jnp.arange(count, dtype=jnp.int32)
    phase = grid[:, None] * grid[None, :] % count
    angle = phase.astype(jnp.float32) * (2.0 * math.pi / count)
    return (jnp.cos(angle) + jnp.sin(angle)) / math.sqrt(count)


def along_first(table, field):
    return jnp.einsum("tk,kqn->tqn", table, field, precision=HIGH)


def along_second(table, field):
    return jnp.einsum("sq,tqn->tsn", table, field, precision=HIGH)


def band_matrix(masked, band_code, nodes):
    blocks = nodes // NB
    reach = HALO_B * NB
    offsets = jnp.arange(NOFF, dtype=jnp.int32)
    select = (offsets[:, None] == band_code[None, :]).astype(jnp.float32)
    per_offset = jnp.einsum("oj,bjsc->obsc", select, masked, precision=HIGH)
    diagonal = jnp.eye(blocks, dtype=jnp.float32)
    operator = jnp.zeros((nodes + 2 * reach, nodes), dtype=jnp.float32)
    for offset in range(NOFF):
        placed = jnp.einsum("bsc,bd->bcds", per_offset[offset], diagonal).reshape(nodes, nodes)
        operator = operator.at[offset * NB : offset * NB + nodes].add(placed)
    return operator


def couple(field, operator, scale):
    reach = HALO_B * NB
    padded = extended(field, (("node", 2),), reach)
    rows = field.shape[0] * field.shape[1]
    term = jnp.dot(padded.reshape(rows, padded.shape[2]), operator, precision=HIGH)
    return scale * field + term.reshape(field.shape)


def small_solve(gram, rhs):
    lower = jnp.linalg.cholesky(gram)
    count = rhs.shape[0]
    forward = []
    for index in range(count):
        total = rhs[index]
        for other in range(index):
            total = total - lower[index, other] * forward[other]
        forward.append(total / lower[index, index])
    backward = [None] * count
    for index in reversed(range(count)):
        total = forward[index]
        for other in range(index + 1, count):
            total = total - lower[other, index] * backward[other]
        backward[index] = total / lower[index, index]
    return jnp.stack(backward)


def per_device(voltages, source, coupling, band_code, active, cap, damp, kind, type_params):
    first = hartley(K1)
    second = hartley(K2)
    onehot = (kind[None, :] == jnp.arange(NTYPES, dtype=jnp.int32)[:, None]).astype(jnp.float32)
    per_node = jnp.dot(type_params, onehot, precision=HIGH)
    masked = coupling * active[:, :, None, None].astype(jnp.float32)
    operator = band_matrix(masked, band_code, voltages.shape[2])
    scale = damp[:, :, None] * cap[None, None, :]

    def to_time(field):
        moved = lax.all_to_all(
            along_first(first, field), "tone", split_axis=0, concat_axis=1, tiled=True
        )
        return along_second(second, moved)

    def to_freq(field):
        moved = lax.all_to_all(
            along_second(second, field), "tone", split_axis=1, concat_axis=0, tiled=True
        )
        return along_first(first, moved)

    linear, amplitude, sharpness = (per_node[0], per_node[1], per_node[2])
    wave = to_time(voltages)
    bend = jnp.tanh(sharpness * wave)
    current = linear * wave + amplitude * bend
    slope = linear + amplitude * sharpness * (1.0 - bend * bend)
    start = source - couple(voltages, operator, scale) - to_freq(current)
    beta = jnp.sqrt(lax.psum(jnp.sum(start * start), ("node", "tone")))
    basis = [start / beta]
    hessen = jnp.zeros((M + 1, M), dtype=jnp.float32)
    for column in range(M):
        jacobian_field = basis[column]
        image = couple(jacobian_field, operator, scale) + to_freq(slope * to_time(jacobian_field))
        local_terms = jnp.stack([jnp.sum(vector * image) for vector in basis])
        projected = lax.psum(local_terms, ("node", "tone"))
        for index in range(len(basis)):
            image = image - projected[index] * basis[index]
        length = jnp.sqrt(lax.psum(jnp.sum(image * image), ("node", "tone")))
        hessen = hessen.at[: column + 1, column].set(projected)
        hessen = hessen.at[column + 1, column].set(length)
        basis.append(image / length)
    gram = jnp.dot(hessen.T, hessen, precision=HIGH)
    coeffs = small_solve(gram, beta * hessen[0])
    fitted = jnp.dot(hessen, coeffs, precision=HIGH)
    update = coeffs[0] * basis[0]
    for index in range(1, M):
        update = update + coeffs[index] * basis[index]
    remaining = start
    for index in range(M + 1):
        remaining = remaining - fitted[index] * basis[index]
    return (voltages + update, remaining)


def solution(mesh):
    placed = (
        P(None, "tone", "node"),
        P(None, "tone", "node"),
        P("node", None, None, None),
        P(),
        P("node", None),
        P("node"),
        P(None, "tone"),
        P("node"),
        P(),
    )
    return jax.shard_map(
        per_device,
        mesh=mesh,
        in_specs=placed,
        out_specs=(P(None, "tone", "node"), P(None, "tone", "node")),
        check_vma=False,
    )
```

profile of v0, /device:TPU:0, one launch (start us, length us, event | category | flops | bytes accessed | tf_op | source)
XLA Modules:
  0.0 942.5 jit_solution(3432726177361847667)
XLA Ops:
  33.9 9.7 %broadcast_multiply_fusion = (f32[8,8,128,128]{2,1,3,0:T(8,128)}, f32[8,8,128,128]{2,1,3,0:T(8,128)}, f32[8,8,128,128]{2,1,3,0:T(8,128)}, f32[8,8,128,128]{2,1,3...) fusion(f32[8,128,128]{1,2,0:T(8,128)} %copy.111, ...), kind=kLoop, calls=%fused_computation.116 | loop fusion | flops 7340032 | bytes 33030400 | tf_op jit(solution)/shard_map/bsc,bd->bcds/dot_general | solution.py:54
  46.8 6.3 scatter-add.24
  64.9 5.9 fusion.13
  89.8 7.2 fusion.11
  102.7 12.3 %all-to-all-done.1 = f32[16,32,1024]{2,0,1:T(8,128)S(1)} async-done(((f32[16,32,1024]{2,0,1:T(8,128)}), f32[16,32,1024]{2,0,1:T(8,128)S(1)}, u32[]{:S(2)}, u32[]{:S(2)}) %all-to-all-start.1) | async-done | bytes 2097184 | tf_op jit(solution)/shard_map/all_to_all | solution.py:101
  117.3 17.0 %multiply_reduce_fusion.14 = (f32[]{:T(128)}, f32[32,16,1024]{2,1,0:T(8,128)S(1)}) fusion(f32[32,16,1024]{2,0,1:T(8,128)S(1)} %fusion.146, f32[32,16,1024]{2,1,0:T(8,128)S(1)} %copy-done.30, f32[1792,1024]{1,0:T(8,128)} %fusion.10, f32[32,16,384]{2,1,0:T(8,128)} %collective-permute-done.1, f32[32,16,1024]{2,1,0:T(8,128)S(1)} %copy-done.16, ...), kind=kOutput, calls=%fused_computation.111 | convolution fusion | flops 11279794176 | bytes 17307652 | tf_op jit(solution)/shard_map/dot_general | solution.py:63
  134.3 42.4 %psum.63 = f32[]{:T(128)} all-reduce(f32[]{:T(128)} %get-tuple-element.256), channel_id=1, replica_groups=mesh['node'=16,'tone'=2] {'node','tone'}, use_global_device_ids=true, to_apply=%region_1.2 | all-reduce | flops 1 | bytes 8 | tf_op jit(solution)/shard_map/psum | solution.py:112
  188.2 25.1 %all-to-all-done.2 = f32[32,16,1024]{2,1,0:T(8,128)} async-done(((f32[32,16,1024]{2,1,0:T(8,128)}), f32[32,16,1024]{2,1,0:T(8,128)}, u32[]{:S(2)}, u32[]{:S(2)}) %all-to-all-start.2) | async-done | bytes 2097184 | tf_op jit(solution)/shard_map/all_to_all | solution.py:95
  233.6 17.5 %all-to-all-done.3 = f32[16,32,1024]{2,0,1:T(8,128)} async-done(((f32[16,32,1024]{2,0,1:T(8,128)}), f32[16,32,1024]{2,0,1:T(8,128)}, u32[]{:S(2)}, u32[]{:S(2)}) %all-to-all-start.3) | async-done | bytes 2097184 | tf_op jit(solution)/shard_map/all_to_all | solution.py:101
  254.8 17.5 %multiply_reduce_fusion.13 = (f32[]{:T(128)}, f32[32,16,1024]{2,1,0:T(8,128)}) fusion(f32[32,16,1024]{2,1,0:T(8,128)S(1)} %get-tuple-element.257, f32[]{:T(128)S(6)} %sqrt.15, f32[32,16,1024]{2,0,1:T(8,128)S(1)} %fusion.140, f32[1792,1024]{1,0:T(8,128)} %fusion.10, f32[32,16,384]{2,1,0:T(8,128)} %collective-permute-done.3, ...), kind=kOutput, calls=%fused_computation.110 | convolution fusion | flops 11279794176 | bytes 17307656 | tf_op jit(solution)/shard_map/dot_general | solution.py:63
  272.3 38.9 %psum.64 = f32[1]{0:T(128)} all-reduce(f32[1]{0:T(128)} %bitcast.38), channel_id=1, replica_groups=mesh['node'=16,'tone'=2] {'node','tone'}, use_global_device_ids=true, to_apply=%region_3.4 | all-reduce | flops 1 | bytes 8 | tf_op jit(solution)/shard_map/psum | solution.py:119
  314.6 41.2 %psum.65 = f32[]{:T(128)} all-reduce(f32[]{:T(128)} %multiply_reduce_fusion.12), channel_id=1, replica_groups=mesh['node'=16,'tone'=2] {'node','tone'}, use_global_device_ids=true, to_apply=%region_5.6 | all-reduce | flops 1 | bytes 8 | tf_op jit(solution)/shard_map/psum | solution.py:122
  363.6 27.1 %all_to_all.180 = f32[32,16,1024]{2,1,0:T(8,128)S(1)} all-to-all(f32[32,16,1024]{2,1,0:T(8,128)S(1)} %copy.125), channel_id=1, replica_groups=mesh['node'=16,'tone'=2] {'tone'}, dimensions={0} | all-to-all | bytes 4194304 | tf_op jit(solution)/shard_map/all_to_all | solution.py:95
  409.3 16.6 %all-to-all-done.5 = f32[16,32,1024]{2,0,1:T(8,128)} async-done(((f32[16,32,1024]{2,0,1:T(8,128)}), f32[16,32,1024]{2,0,1:T(8,128)}, u32[]{:S(2)}, u32[]{:S(2)}) %all-to-all-start.5) | async-done | bytes 2097184 | tf_op jit(solution)/shard_map/all_to_all | solution.py:101
  429.6 17.6 %multiply_reduce_fusion.11 = (f32[]{:T(128)}, f32[]{:T(128)}, f32[32,16,1024]{2,1,0:T(8,128)}) fusion(f32[32,16,1024]{2,1,0:T(8,128)S(1)} %get-tuple-element.257, f32[]{:T(128)S(6)} %sqrt.15, f32[32,16,1024]{2,1,0:T(8,128)S(1)} %copy-done.3, f32[32,16,1024]{2,0,1:T(8,128)S(1)} %fusion.134, f32[1792,1024]{1,0:T(8,128)} %fusion.10, ...), kind=kOutput, calls=%fused_computation.107 | convolution fusion | flops 11280842752 | bytes 17307660 | tf_op jit(solution)/shard_map/dot_general | solution.py:63
  448.6 38.6 %psum.66 = f32[2]{0:T(128)S(1)} all-reduce(f32[2]{0:T(128)S(1)} %pad_maximum_fusion), channel_id=1, replica_groups=mesh['node'=16,'tone'=2] {'node','tone'}, use_global_device_ids=true, to_apply=%region_9.10 | all-reduce | flops 2 | bytes 16 | tf_op jit(solution)/shard_map/psum | solution.py:119
  487.8 6.2 multiply_reduce_fusion.9
  494.1 40.7 %psum.67 = f32[]{:T(128)} all-reduce(f32[]{:T(128)} %get-tuple-element.193), channel_id=1, replica_groups=mesh['node'=16,'tone'=2] {'node','tone'}, use_global_device_ids=true, to_apply=%region_11.12 | all-reduce | flops 1 | bytes 8 | tf_op jit(solution)/shard_map/psum | solution.py:122
  541.5 27.1 %all_to_all.181 = f32[32,16,1024]{2,1,0:T(8,128)S(1)} all-to-all(f32[32,16,1024]{2,1,0:T(8,128)S(1)} %copy.131), channel_id=1, replica_groups=mesh['node'=16,'tone'=2] {'tone'}, dimensions={0} | all-to-all | bytes 4194304 | tf_op jit(solution)/shard_map/all_to_all | solution.py:95
  587.1 16.7 %all-to-all-done.7 = f32[16,32,1024]{2,0,1:T(8,128)} async-done(((f32[16,32,1024]{2,0,1:T(8,128)}), f32[16,32,1024]{2,0,1:T(8,128)}, u32[]{:S(2)}, u32[]{:S(2)}) %all-to-all-start.7) | async-done | bytes 2097184 | tf_op jit(solution)/shard_map/all_to_all | solution.py:101
  607.7 17.6 %multiply_reduce_fusion.8 = (f32[]{:T(128)}, f32[]{:T(128)}, f32[]{:T(128)}, f32[32,16,1024]{2,1,0:T(8,128)}) fusion(f32[32,16,1024]{2,1,0:T(8,128)S(1)} %get-tuple-element.257, f32[]{:T(128)S(6)} %sqrt.15, f32[32,16,1024]{2,1,0:T(8,128)S(1)} %copy-done.23, f32[32,16,1024]{2,1,0:T(8,128)S(1)} %copy-done.4, f32[32,16,1024]{2,0,1:T(8,128)S(1)} %fusion.128, ...), kind=kOutput, calls=%fused_computation.103 | convolution fusion | flops 11281891328 | bytes 19404816 | tf_op jit(solution)/shard_map/dot_general | solution.py:63
  627.3 38.9 %psum.68 = f32[3]{0:T(128)S(1)} all-reduce(f32[3]{0:T(128)S(1)} %pad_maximum_fusion.1), channel_id=1, replica_groups=mesh['node'=16,'tone'=2] {'node','tone'}, use_global_device_ids=true, to_apply=%region_16.17 | all-reduce | flops 3 | bytes 24 | tf_op jit(solution)/shard_map/psum | solution.py:119
  666.8 7.7 multiply_reduce_fusion.5
  674.5 41.0 %psum.69 = f32[]{:T(128)} all-reduce(f32[]{:T(128)} %get-tuple-element.191), channel_id=1, replica_groups=mesh['node'=16,'tone'=2] {'node','tone'}, use_global_device_ids=true, to_apply=%region_18.19 | all-reduce | flops 1 | bytes 8 | tf_op jit(solution)/shard_map/psum | solution.py:122
  730.6 22.6 %all-to-all-done.8 = f32[32,16,1024]{2,1,0:T(8,128)} async-done(((f32[32,16,1024]{2,1,0:T(8,128)}), f32[32,16,1024]{2,1,0:T(8,128)}, u32[]{:S(2)}, u32[]{:S(2)}) %all-to-all-start.8) | async-done | bytes 2097184 | tf_op jit(solution)/shard_map/all_to_all | solution.py:95
  781.5 9.0 all-to-all-done.9
  794.9 18.1 %multiply_reduce_fusion.4 = (f32[]{:T(128)}, f32[]{:T(128)}, f32[]{:T(128)}, f32[]{:T(128)}, f32[32,16,1024]{2,1,0:T(8,128)}) fusion(f32[32,16,1024]{2,1,0:T(8,128)S(1)} %get-tuple-element.257, f32[]{:T(128)S(6)} %sqrt.15, f32[32,16,1024]{2,1,0:T(8,128)S(1)} %copy-done.13, f32[]{:T(128)} %sqrt.18, f32[32,16,1024]{2,1,0:T(8,128)S(1)} %copy-done.24, ...), kind=kOutput, calls=%fused_computation.98 | convolution fusion | flops 11283464192 | bytes 23599128 | tf_op jit(solution)/shard_map/dot_general | solution.py:63
  817.0 38.6 %psum.70 = f32[4]{0:T(128)S(1)} all-reduce(f32[4]{0:T(128)S(1)} %pad_maximum_fusion.2), channel_id=1, replica_groups=mesh['node'=16,'tone'=2] {'node','tone'}, use_global_device_ids=true, to_apply=%region_24.25 | all-reduce | flops 4 | bytes 32 | tf_op jit(solution)/shard_map/psum | solution.py:119
  856.3 7.6 multiply_reduce_fusion
  864.0 39.6 %psum.71 = f32[]{:T(128)} all-reduce(f32[]{:T(128)} %multiply_reduce_fusion), channel_id=1, replica_groups=mesh['node'=16,'tone'=2] {'node','tone'}, use_global_device_ids=true, to_apply=%region_26.27 | all-reduce | flops 1 | bytes 8 | tf_op jit(solution)/shard_map/psum | solution.py:122
  926.7 6.5 add_add_fusion
  934.1 8.2 multiply_subtract_fusion
  (214 shorter events, 234.6 us)
Async XLA Ops:
  0.6 46.0 %copy-start = (f32[3,4]{1,0:T(4,128)S(1)}, f32[3,4]{1,0:T(4,128)}, u32[]{:S(2)}) copy-start(f32[3,4]{1,0:T(4,128)} %param.47) | copy-start | bytes 148
  7.8 5.0 copy-start.15
  7.8 68.8 %all-to-all-start = ((f32[32,16,1024]{2,1,0:T(8,128)}), f32[32,16,1024]{2,1,0:T(8,128)}, u32[]{:S(2)}, u32[]{:S(2)}) async-start(f32[32,16,1024]{2,1,0:T(8,128)} %copy.113), calls=%async_computation | async-start | bytes 4194304 | tf_op jit(solution)/shard_map/all_to_all | solution.py:95
  12.8 6.2 copy-start.32
  14.1 103.0 %collective-permute-start = (f32[32,16,384]{2,1,0:T(8,128)}, f32[32,16,384]{2,1,0:T(8,128)}, u32[]{:S(2)}, u32[]{:S(2)}) collective-permute-start(f32[32,16,384]{2,1,0:T(8,128)} %get-tuple-element.210), channel_id=1, source_target_pairs={{0,2},{2,4},{4,6},{6,8},{8,10},{10,12},{12,14},{14,16},{16,18},{18... | collective-permute-start | bytes 2359304 | tf_op jit(solution)/shard_map/ppermute | solution.py:24
  17.4 99.7 %collective-permute-start.1 = (f32[32,16,384]{2,1,0:T(8,128)}, f32[32,16,384]{2,1,0:T(8,128)}, u32[]{:S(2)}, u32[]{:S(2)}) collective-permute-start(f32[32,16,384]{2,1,0:T(8,128)} %get-tuple-element.211), channel_id=1, source_target_pairs={{2,0},{4,2},{6,4},{8,6},{10,8},{12,10},{14,12},{16,14},{18,16},{20... | collective-permute-start | bytes 2359304 | tf_op jit(solution)/shard_map/ppermute | solution.py:25
  46.8 6.3 copy-start.21
  53.2 5.8 copy-start.20
  59.0 5.9 copy-start.19
  64.9 5.9 copy-start.18
  86.0 28.9 %all-to-all-start.1 = ((f32[16,32,1024]{2,0,1:T(8,128)}), f32[16,32,1024]{2,0,1:T(8,128)S(1)}, u32[]{:S(2)}, u32[]{:S(2)}) async-start(f32[16,32,1024]{2,0,1:T(8,128)} %copy.115), calls=%async_computation.1 | async-start | bytes 4194304 | tf_op jit(solution)/shard_map/all_to_all | solution.py:101
  89.8 7.2 copy-start.17
  183.2 30.2 %all-to-all-start.2 = ((f32[32,16,1024]{2,1,0:T(8,128)}), f32[32,16,1024]{2,1,0:T(8,128)}, u32[]{:S(2)}, u32[]{:S(2)}) async-start(f32[32,16,1024]{2,1,0:T(8,128)} %copy.119), calls=%async_computation.2 | async-start | bytes 4194304 | tf_op jit(solution)/shard_map/all_to_all | solution.py:95
  222.5 28.6 %all-to-all-start.3 = ((f32[16,32,1024]{2,0,1:T(8,128)}), f32[16,32,1024]{2,0,1:T(8,128)}, u32[]{:S(2)}, u32[]{:S(2)}) async-start(f32[16,32,1024]{2,0,1:T(8,128)} %copy.121), calls=%async_computation.3 | async-start | bytes 4194304 | tf_op jit(solution)/shard_map/all_to_all | solution.py:101
  229.7 25.1 %collective-permute-start.2 = (f32[32,16,384]{2,1,0:T(8,128)}, f32[32,16,384]{2,1,0:T(8,128)}, u32[]{:S(2)}, u32[]{:S(2)}) collective-permute-start(f32[32,16,384]{2,1,0:T(8,128)} %get-tuple-element.208), channel_id=1, source_target_pairs={{0,2},{2,4},{4,6},{6,8},{8,10},{10,12},{12,14},{14,16},{16,18},{18... | collective-permute-start | bytes 2359304 | tf_op jit(solution)/shard_map/ppermute | solution.py:24
  231.9 22.9 %collective-permute-start.3 = (f32[32,16,384]{2,1,0:T(8,128)S(1)}, f32[32,16,384]{2,1,0:T(8,128)}, u32[]{:S(2)}, u32[]{:S(2)}) collective-permute-start(f32[32,16,384]{2,1,0:T(8,128)S(1)} %get-tuple-element.209), channel_id=1, source_target_pairs={{2,0},{4,2},{6,4},{8,6},{10,8},{12,10},{14,12},{16,14},{18,16},{20... | collective-permute-start | bytes 2359304 | tf_op jit(solution)/shard_map/ppermute | solution.py:25
  398.4 27.6 %all-to-all-start.5 = ((f32[16,32,1024]{2,0,1:T(8,128)}), f32[16,32,1024]{2,0,1:T(8,128)}, u32[]{:S(2)}, u32[]{:S(2)}) async-start(f32[16,32,1024]{2,0,1:T(8,128)} %copy.127), calls=%async_computation.5 | async-start | bytes 4194304 | tf_op jit(solution)/shard_map/all_to_all | solution.py:101
  405.6 24.0 %collective-permute-start.4 = (f32[32,16,384]{2,1,0:T(8,128)}, f32[32,16,384]{2,1,0:T(8,128)}, u32[]{:S(2)}, u32[]{:S(2)}) collective-permute-start(f32[32,16,384]{2,1,0:T(8,128)} %get-tuple-element.206), channel_id=1, source_target_pairs={{0,2},{2,4},{4,6},{6,8},{8,10},{10,12},{12,14},{14,16},{16,18},{18... | collective-permute-start | bytes 2359304 | tf_op jit(solution)/shard_map/ppermute | solution.py:24
  407.8 21.8 %collective-permute-start.5 = (f32[32,16,384]{2,1,0:T(8,128)S(1)}, f32[32,16,384]{2,1,0:T(8,128)}, u32[]{:S(2)}, u32[]{:S(2)}) collective-permute-start(f32[32,16,384]{2,1,0:T(8,128)S(1)} %get-tuple-element.207), channel_id=1, source_target_pairs={{2,0},{4,2},{6,4},{8,6},{10,8},{12,10},{14,12},{16,14},{18,16},{20... | collective-permute-start | bytes 2359304 | tf_op jit(solution)/shard_map/ppermute | solution.py:25
  576.2 27.5 %all-to-all-start.7 = ((f32[16,32,1024]{2,0,1:T(8,128)}), f32[16,32,1024]{2,0,1:T(8,128)}, u32[]{:S(2)}, u32[]{:S(2)}) async-start(f32[16,32,1024]{2,0,1:T(8,128)} %copy.133), calls=%async_computation.7 | async-start | bytes 4194304 | tf_op jit(solution)/shard_map/all_to_all | solution.py:101
  583.4 24.0 %collective-permute-start.6 = (f32[32,16,384]{2,1,0:T(8,128)}, f32[32,16,384]{2,1,0:T(8,128)}, u32[]{:S(2)}, u32[]{:S(2)}) collective-permute-start(f32[32,16,384]{2,1,0:T(8,128)} %get-tuple-element.204), channel_id=1, source_target_pairs={{0,2},{2,4},{4,6},{6,8},{8,10},{10,12},{12,14},{14,16},{16,18},{18... | collective-permute-start | bytes 2359304 | tf_op jit(solution)/shard_map/ppermute | solution.py:24
  585.6 21.9 %collective-permute-start.7 = (f32[32,16,384]{2,1,0:T(8,128)S(1)}, f32[32,16,384]{2,1,0:T(8,128)}, u32[]{:S(2)}, u32[]{:S(2)}) collective-permute-start(f32[32,16,384]{2,1,0:T(8,128)S(1)} %get-tuple-element.205), channel_id=1, source_target_pairs={{2,0},{4,2},{6,4},{8,6},{10,8},{12,10},{14,12},{16,14},{18,16},{20... | collective-permute-start | bytes 2359304 | tf_op jit(solution)/shard_map/ppermute | solution.py:25
  723.6 6.3 copy-start.37
  723.6 29.5 %all-to-all-start.8 = ((f32[32,16,1024]{2,1,0:T(8,128)}), f32[32,16,1024]{2,1,0:T(8,128)}, u32[]{:S(2)}, u32[]{:S(2)}) async-start(f32[32,16,1024]{2,1,0:T(8,128)} %copy.137), calls=%async_computation.8 | async-start | bytes 4194304 | tf_op jit(solution)/shard_map/all_to_all | solution.py:95
  762.3 28.2 %all-to-all-start.9 = ((f32[16,32,1024]{2,0,1:T(8,128)}), f32[16,32,1024]{2,0,1:T(8,128)}, u32[]{:S(2)}, u32[]{:S(2)}) async-start(f32[16,32,1024]{2,0,1:T(8,128)} %copy.139), calls=%async_computation.9 | async-start | bytes 4194304 | tf_op jit(solution)/shard_map/all_to_all | solution.py:101
  770.4 24.0 %collective-permute-start.8 = (f32[32,16,384]{2,1,0:T(8,128)}, f32[32,16,384]{2,1,0:T(8,128)}, u32[]{:S(2)}, u32[]{:S(2)}) collective-permute-start(f32[32,16,384]{2,1,0:T(8,128)} %get-tuple-element.202), channel_id=1, source_target_pairs={{0,2},{2,4},{4,6},{6,8},{8,10},{10,12},{12,14},{14,16},{16,18},{18... | collective-permute-start | bytes 2359304 | tf_op jit(solution)/shard_map/ppermute | solution.py:24
  772.5 21.9 %collective-permute-start.9 = (f32[32,16,384]{2,1,0:T(8,128)S(1)}, f32[32,16,384]{2,1,0:T(8,128)}, u32[]{:S(2)}, u32[]{:S(2)}) collective-permute-start(f32[32,16,384]{2,1,0:T(8,128)S(1)} %get-tuple-element.203), channel_id=1, source_target_pairs={{2,0},{4,2},{6,4},{8,6},{10,8},{12,10},{14,12},{16,14},{18,16},{20... | collective-permute-start | bytes 2359304 | tf_op jit(solution)/shard_map/ppermute | solution.py:25
  926.7 7.4 copy-start.6
  926.7 7.4 copy-start.12
  926.7 7.4 copy-start.14
  926.7 7.4 copy-start.29
  934.1 8.2 copy-start.1
  (24 other events, 64.1 us)
where the time goes:
time: 949 us; the launch traced here: 942 us
  blocking collectives  414 us (44%)
  matrix products  143 us (15%)
  waiting for transfers between devices  120 us (13%)
  other arithmetic  110 us (12%)
  local copies, waits for them, and re-layouts  77 us (8%)
  starting transfers between devices  57.6 us (6%)
  between operations  20.7 us (2%)
    psum x4, blocking collectives, per_device(): length = jnp.sqrt(lax.psum(jnp.sum(image * image), ('node', 'tone')))  163 us
    psum x4, blocking collectives, per_device(): projected = lax.psum(local_terms, ('node', 'tone'))  155 us
    dot_general x5, matrix products, couple(): jnp.dot(padded.reshape(rows, padded.shape[2]), operator, precision=HIGH)  87.9 us
    all_to_all x5, waiting for transfers between devices, to_freq(): lax.all_to_all(along_second(second, field), 'tone', split_axis=1, concat_...  72.1 us
    all_to_all x2, blocking collectives, to_time(): lax.all_to_all(along_first(first, field), 'tone', split_axis=0, concat_ax...  54.2 us
    all_to_all x3, waiting for transfers between devices, to_time(): lax.all_to_all(along_first(first, field), 'tone', split_axis=0, concat_ax...  47.7 us
    psum x1, blocking collectives, per_device(): beta = jnp.sqrt(lax.psum(jnp.sum(start * start), ('node', 'tone')))  42.4 us
    scatter-add x6, other arithmetic, band_matrix(): operator = operator.at[offset * NB:offset * NB + nodes].add(placed)  36.2 us
  transfers between devices with their start and end apart: 18, of which 7 were waited for; matrix products, arithmetic and copies ran while one was open for 13% of the time, Pallas kernels for 0%

commit v1 on v0

--- a/solution.py
+++ b/solution.py
@@ -98,8 +98,14 @@
         return along_second(second, moved)
 
     def to_freq(field):
-        moved = lax.all_to_all(
-            along_second(second, field), "tone", split_axis=1, concat_axis=0, tiled=True
+        moved = jnp.concatenate(
+            lax.all_to_all(
+                jnp.stack(jnp.split(along_second(second, field), lax.axis_size("tone"), axis=1)),
+                "tone",
+                0,
+                0,
+            ),
+            axis=0,
         )
         return along_first(first, moved)
 

time: 949 us -> 951 us (level)
  local copies, waits for them, and re-layouts: 77 us -> 58.3 us
  matrix products: 143 us -> 157 us
    transpose x5 -> x0, local copies, waits for them, and re-layouts: 12.7 us -> none  [along_second(): return jnp.einsum('sq,tqn->tsn', table, field, precision=HIGH)]
    dot_general x10, matrix products: 26.4 us -> 38.7 us  [along_first(): return jnp.einsum('tk,kqn->tqn', table, field, precision=HIGH)]
where the time goes in v1:
time: 951 us; the launch traced here: 945 us
  blocking collectives  414 us (44%)
  matrix products  157 us (17%)
  waiting for transfers between devices  120 us (13%)
  other arithmetic  117 us (12%)
  local copies, waits for them, and re-layouts  58.3 us (6%)
  starting transfers between devices  57.3 us (6%)
  between operations  20.5 us (2%)
    psum x4, blocking collectives, per_device(): length = jnp.sqrt(lax.psum(jnp.sum(image * image), ('node', 'tone')))  163 us
    psum x4, blocking collectives, per_device(): projected = lax.psum(local_terms, ('node', 'tone'))  155 us
    dot_general x5, matrix products, couple(): jnp.dot(padded.reshape(rows, padded.shape[2]), operator, precision=HIGH)  89.3 us
    all_to_all x5, waiting for transfers between devices, to_freq(): lax.all_to_all(jnp.stack(jnp.split(along_second(second, field), lax.axis_...  72.5 us
    all_to_all x2, blocking collectives, to_time(): lax.all_to_all(along_first(first, field), 'tone', split_axis=0, concat_ax...  54.1 us
    all_to_all x3, waiting for transfers between devices, to_time(): lax.all_to_all(along_first(first, field), 'tone', split_axis=0, concat_ax...  47.9 us
    psum x1, blocking collectives, per_device(): beta = jnp.sqrt(lax.psum(jnp.sum(start * start), ('node', 'tone')))  42.5 us
    dot_general x10, matrix products, along_first(): return jnp.einsum('tk,kqn->tqn', table, field, precision=HIGH)  38.7 us
  transfers between devices with their start and end apart: 18, of which 7 were waited for; matrix products, arithmetic and copies ran while one was open for 13% of the time, Pallas kernels for 0%

profile of v1, /device:TPU:0, one launch (start us, length us, event | category | flops | bytes accessed | tf_op | source)
XLA Modules:
  0.0 944.5 jit_solution(297518831957517880)
XLA Ops:
  33.9 9.7 %broadcast_multiply_fusion = (f32[8,8,128,128]{2,1,3,0:T(8,128)}, f32[8,8,128,128]{2,1,3,0:T(8,128)}, f32[8,8,128,128]{2,1,3,0:T(8,128)}, f32[8,8,128,128]{2,1,3...) fusion(f32[8,128,128]{1,2,0:T(8,128)} %copy.106, ...), kind=kLoop, calls=%fused_computation.131 | loop fusion | flops 7340032 | bytes 33030400 | tf_op jit(solution)/shard_map/bsc,bd->bcds/dot_general | solution.py:54
  46.9 6.3 scatter-add.24
  64.9 5.9 fusion.13
  90.5 7.2 fusion.11
  103.4 12.2 %all-to-all-done.1 = f32[2,16,16,1024]{3,2,1,0:T(8,128)S(1)} async-done(((f32[2,16,16,1024]{3,2,1,0:T(8,128)}), f32[2,16,16,1024]{3,2,1,0:T(8,128)S(1)}, u32[]{:S(2)}, u32[]{:S(2)}) %all-to-all-start.1) | async-done | bytes 2097184 | tf_op jit(solution)/shard_map/all_to_all | solution.py:102
  118.7 17.1 %multiply_reduce_fusion.14 = (f32[]{:T(128)}, f32[32,16,1024]{2,1,0:T(8,128)S(1)}) fusion(f32[32,16,1024]{2,0,1:T(8,128)S(1)} %fusion.80, f32[32,16,1024]{2,1,0:T(8,128)S(1)} %copy-done.28, f32[1792,1024]{1,0:T(8,128)} %fusion.10, f32[32,16,384]{2,1,0:T(8,128)} %collective-permute-done.1, f32[32,16,1024]{2,1,0:T(8,128)S(1)} %copy-done.16, ...), kind=kOutput, calls=%fused_computation.126 | convolution fusion | flops 11279794176 | bytes 17307652 | tf_op jit(solution)/shard_map/dot_general | solution.py:63
  135.8 42.5 %psum.63 = f32[]{:T(128)} all-reduce(f32[]{:T(128)} %get-tuple-element.266), channel_id=1, replica_groups=mesh['node'=16,'tone'=2] {'node','tone'}, use_global_device_ids=true, to_apply=%region_1.2 | all-reduce | flops 1 | bytes 8 | tf_op jit(solution)/shard_map/psum | solution.py:118
  190.0 25.2 %all-to-all-done.2 = f32[32,16,1024]{2,1,0:T(8,128)} async-done(((f32[32,16,1024]{2,1,0:T(8,128)}), f32[32,16,1024]{2,1,0:T(8,128)}, u32[]{:S(2)}, u32[]{:S(2)}) %all-to-all-start.2) | async-done | bytes 2097184 | tf_op jit(solution)/shard_map/all_to_all | solution.py:95
  234.1 18.0 %all-to-all-done.3 = f32[2,16,16,1024]{3,2,1,0:T(8,128)} async-done(((f32[2,16,16,1024]{3,2,1,0:T(8,128)}), f32[2,16,16,1024]{3,2,1,0:T(8,128)}, u32[]{:S(2)}, u32[]{:S(2)}) %all-to-all-start.3) | async-done | bytes 2097184 | tf_op jit(solution)/shard_map/all_to_all | solution.py:102
  256.9 17.4 %multiply_reduce_fusion.13 = (f32[]{:T(128)}, f32[32,16,1024]{2,1,0:T(8,128)}) fusion(f32[32,16,1024]{2,1,0:T(8,128)S(1)} %get-tuple-element.267, f32[]{:T(128)S(6)} %sqrt.15, f32[32,16,1024]{2,0,1:T(8,128)S(1)} %fusion.76, f32[1792,1024]{1,0:T(8,128)} %fusion.10, f32[32,16,384]{2,1,0:T(8,128)} %collective-permute-done.3, ...), kind=kOutput, calls=%fused_computation.125 | convolution fusion | flops 11279794176 | bytes 17307656 | tf_op jit(solution)/shard_map/dot_general | solution.py:63
  274.3 38.9 %psum.64 = f32[1]{0:T(128)} all-reduce(f32[1]{0:T(128)} %bitcast.38), channel_id=1, replica_groups=mesh['node'=16,'tone'=2] {'node','tone'}, use_global_device_ids=true, to_apply=%region_3.4 | all-reduce | flops 1 | bytes 8 | tf_op jit(solution)/shard_map/psum | solution.py:125
  316.5 41.1 %psum.65 = f32[]{:T(128)} all-reduce(f32[]{:T(128)} %multiply_reduce_fusion.12), channel_id=1, replica_groups=mesh['node'=16,'tone'=2] {'node','tone'}, use_global_device_ids=true, to_apply=%region_5.6 | all-reduce | flops 1 | bytes 8 | tf_op jit(solution)/shard_map/psum | solution.py:128
  365.2 27.0 %all_to_all.115 = f32[32,16,1024]{2,1,0:T(8,128)S(1)} all-to-all(f32[32,16,1024]{2,1,0:T(8,128)S(1)} %copy.118), channel_id=1, replica_groups=mesh['node'=16,'tone'=2] {'tone'}, dimensions={0} | all-to-all | bytes 4194304 | tf_op jit(solution)/shard_map/all_to_all | solution.py:95
  409.9 16.6 %all-to-all-done.5 = f32[2,16,16,1024]{3,2,1,0:T(8,128)} async-done(((f32[2,16,16,1024]{3,2,1,0:T(8,128)}), f32[2,16,16,1024]{3,2,1,0:T(8,128)}, u32[]{:S(2)}, u32[]{:S(2)}) %all-to-all-start.5) | async-done | bytes 2097184 | tf_op jit(solution)/shard_map/all_to_all | solution.py:102
  431.3 17.6 %multiply_reduce_fusion.11 = (f32[]{:T(128)}, f32[]{:T(128)}, f32[32,16,1024]{2,1,0:T(8,128)}) fusion(f32[32,16,1024]{2,1,0:T(8,128)S(1)} %get-tuple-element.267, f32[]{:T(128)S(6)} %sqrt.15, f32[32,16,1024]{2,1,0:T(8,128)S(1)} %copy-done.3, f32[32,16,1024]{2,0,1:T(8,128)S(1)} %fusion.72, f32[1792,1024]{1,0:T(8,128)} %fusion.10, ...), kind=kOutput, calls=%fused_computation.122 | convolution fusion | flops 11280842752 | bytes 17307660 | tf_op jit(solution)/shard_map/dot_general | solution.py:63
  450.2 38.6 %psum.66 = f32[2]{0:T(128)S(1)} all-reduce(f32[2]{0:T(128)S(1)} %pad_maximum_fusion.5), channel_id=1, replica_groups=mesh['node'=16,'tone'=2] {'node','tone'}, use_global_device_ids=true, to_apply=%region_9.10 | all-reduce | flops 2 | bytes 16 | tf_op jit(solution)/shard_map/psum | solution.py:125
  489.4 6.1 multiply_reduce_fusion.9
  495.5 40.7 %psum.67 = f32[]{:T(128)} all-reduce(f32[]{:T(128)} %get-tuple-element.193), channel_id=1, replica_groups=mesh['node'=16,'tone'=2] {'node','tone'}, use_global_device_ids=true, to_apply=%region_11.12 | all-reduce | flops 1 | bytes 8 | tf_op jit(solution)/shard_map/psum | solution.py:128
  542.9 27.0 %all_to_all.116 = f32[32,16,1024]{2,1,0:T(8,128)S(1)} all-to-all(f32[32,16,1024]{2,1,0:T(8,128)S(1)} %copy.123), channel_id=1, replica_groups=mesh['node'=16,'tone'=2] {'tone'}, dimensions={0} | all-to-all | bytes 4194304 | tf_op jit(solution)/shard_map/all_to_all | solution.py:95
  587.5 16.7 %all-to-all-done.7 = f32[2,16,16,1024]{3,2,1,0:T(8,128)} async-done(((f32[2,16,16,1024]{3,2,1,0:T(8,128)}), f32[2,16,16,1024]{3,2,1,0:T(8,128)}, u32[]{:S(2)}, u32[]{:S(2)}) %all-to-all-start.7) | async-done | bytes 2097184 | tf_op jit(solution)/shard_map/all_to_all | solution.py:102
  609.0 17.6 %multiply_reduce_fusion.8 = (f32[]{:T(128)}, f32[]{:T(128)}, f32[]{:T(128)}, f32[32,16,1024]{2,1,0:T(8,128)}) fusion(f32[32,16,1024]{2,1,0:T(8,128)S(1)} %get-tuple-element.267, f32[]{:T(128)S(6)} %sqrt.15, f32[32,16,1024]{2,1,0:T(8,128)S(1)} %copy-done.23, f32[32,16,1024]{2,1,0:T(8,128)S(1)} %copy-done.4, f32[32,16,1024]{2,0,1:T(8,128)S(1)} %fusion.68, ...), kind=kOutput, calls=%fused_computation.118 | convolution fusion | flops 11281891328 | bytes 19404816 | tf_op jit(solution)/shard_map/dot_general | solution.py:63
  628.6 38.9 %psum.68 = f32[3]{0:T(128)S(1)} all-reduce(f32[3]{0:T(128)S(1)} %pad_maximum_fusion.6), channel_id=1, replica_groups=mesh['node'=16,'tone'=2] {'node','tone'}, use_global_device_ids=true, to_apply=%region_16.17 | all-reduce | flops 3 | bytes 24 | tf_op jit(solution)/shard_map/psum | solution.py:125
  668.2 7.8 multiply_reduce_fusion.5
  675.9 41.1 %psum.69 = f32[]{:T(128)} all-reduce(f32[]{:T(128)} %get-tuple-element.191), channel_id=1, replica_groups=mesh['node'=16,'tone'=2] {'node','tone'}, use_global_device_ids=true, to_apply=%region_18.19 | all-reduce | flops 1 | bytes 8 | tf_op jit(solution)/shard_map/psum | solution.py:128
  732.0 22.8 %all-to-all-done.8 = f32[32,16,1024]{2,1,0:T(8,128)} async-done(((f32[32,16,1024]{2,1,0:T(8,128)}), f32[32,16,1024]{2,1,0:T(8,128)}, u32[]{:S(2)}, u32[]{:S(2)}) %all-to-all-start.8) | async-done | bytes 2097184 | tf_op jit(solution)/shard_map/all_to_all | solution.py:95
  782.3 9.0 all-to-all-done.9
  796.0 19.5 %multiply_reduce_fusion.4 = (f32[]{:T(128)}, f32[]{:T(128)}, f32[]{:T(128)}, f32[]{:T(128)}, f32[32,16,1024]{2,1,0:T(8,128)}) fusion(f32[32,16,1024]{2,1,0:T(8,128)S(1)} %get-tuple-element.267, f32[]{:T(128)S(6)} %sqrt.15, f32[32,16,1024]{2,1,0:T(8,128)S(1)} %copy-done.13, f32[]{:T(128)} %sqrt.18, f32[32,16,1024]{2,1,0:T(8,128)} %copy-done.22, ...), kind=kOutput, calls=%fused_computation.113 | convolution fusion | flops 11283464192 | bytes 23599128 | tf_op jit(solution)/shard_map/dot_general | solution.py:63
  819.7 38.7 %psum.70 = f32[4]{0:T(128)S(1)} all-reduce(f32[4]{0:T(128)S(1)} %pad_maximum_fusion.7), channel_id=1, replica_groups=mesh['node'=16,'tone'=2] {'node','tone'}, use_global_device_ids=true, to_apply=%region_24.25 | all-reduce | flops 4 | bytes 32 | tf_op jit(solution)/shard_map/psum | solution.py:125
  859.0 7.5 multiply_reduce_fusion
  866.6 40.0 %psum.71 = f32[]{:T(128)} all-reduce(f32[]{:T(128)} %multiply_reduce_fusion), channel_id=1, replica_groups=mesh['node'=16,'tone'=2] {'node','tone'}, use_global_device_ids=true, to_apply=%region_26.27 | all-reduce | flops 1 | bytes 8 | tf_op jit(solution)/shard_map/psum | solution.py:128
  929.1 6.3 add_add_fusion
  936.3 8.0 multiply_subtract_fusion
  (210 shorter events, 235.2 us)
Async XLA Ops:
  0.6 46.0 %copy-start = (f32[3,4]{1,0:T(4,128)S(1)}, f32[3,4]{1,0:T(4,128)}, u32[]{:S(2)}) copy-start(f32[3,4]{1,0:T(4,128)} %param.47) | copy-start | bytes 148
  7.8 68.8 %all-to-all-start = ((f32[32,16,1024]{2,1,0:T(8,128)}), f32[32,16,1024]{2,1,0:T(8,128)}, u32[]{:S(2)}, u32[]{:S(2)}) async-start(f32[32,16,1024]{2,1,0:T(8,128)} %copy.108), calls=%async_computation | async-start | bytes 4194304 | tf_op jit(solution)/shard_map/all_to_all | solution.py:95
  12.8 6.2 copy-start.30
  14.1 104.6 %collective-permute-start = (f32[32,16,384]{2,1,0:T(8,128)}, f32[32,16,384]{2,1,0:T(8,128)}, u32[]{:S(2)}, u32[]{:S(2)}) collective-permute-start(f32[32,16,384]{2,1,0:T(8,128)} %get-tuple-element.218), channel_id=1, source_target_pairs={{0,2},{2,4},{4,6},{6,8},{8,10},{10,12},{12,14},{14,16},{16,18},{18... | collective-permute-start | bytes 2359304 | tf_op jit(solution)/shard_map/ppermute | solution.py:24
  17.4 101.3 %collective-permute-start.1 = (f32[32,16,384]{2,1,0:T(8,128)}, f32[32,16,384]{2,1,0:T(8,128)}, u32[]{:S(2)}, u32[]{:S(2)}) collective-permute-start(f32[32,16,384]{2,1,0:T(8,128)} %get-tuple-element.219), channel_id=1, source_target_pairs={{2,0},{4,2},{6,4},{8,6},{10,8},{12,10},{14,12},{16,14},{18,16},{20... | collective-permute-start | bytes 2359304 | tf_op jit(solution)/shard_map/ppermute | solution.py:25
  46.9 6.3 copy-start.21
  53.2 5.9 copy-start.20
  59.1 5.9 copy-start.19
  64.9 5.9 copy-start.18
  86.7 28.9 %all-to-all-start.1 = ((f32[2,16,16,1024]{3,2,1,0:T(8,128)}), f32[2,16,16,1024]{3,2,1,0:T(8,128)S(1)}, u32[]{:S(2)}, u32[]{:S(2)}) async-start(f32[2,16,16,1024]{3,2,1,0:T(8,128)} %pad_maximum_fusion), calls=%async_computation.1 | async-start | bytes 4194304 | tf_op jit(solution)/shard_map/all_to_all | solution.py:102
  90.5 7.2 copy-start.17
  97.7 21.0 %copy-start.32 = (f32[1024]{0:T(1024)S(1)}, f32[1024]{0:T(1024)}, u32[]{:S(2)}) copy-start(f32[1024]{0:T(1024)} %param.44) | copy-start | bytes 12292
  184.8 30.4 %all-to-all-start.2 = ((f32[32,16,1024]{2,1,0:T(8,128)}), f32[32,16,1024]{2,1,0:T(8,128)}, u32[]{:S(2)}, u32[]{:S(2)}) async-start(f32[32,16,1024]{2,1,0:T(8,128)} %copy.113), calls=%async_computation.2 | async-start | bytes 4194304 | tf_op jit(solution)/shard_map/all_to_all | solution.py:95
  223.5 28.6 %all-to-all-start.3 = ((f32[2,16,16,1024]{3,2,1,0:T(8,128)}), f32[2,16,16,1024]{3,2,1,0:T(8,128)}, u32[]{:S(2)}, u32[]{:S(2)}) async-start(f32[2,16,16,1024]{3,2,1,0:T(8,128)} %pad_maximum_fusion.1), calls=%async_computation.3 | async-start | bytes 4194304 | tf_op jit(solution)/shard_map/all_to_all | solution.py:102
  230.6 26.2 %collective-permute-start.2 = (f32[32,16,384]{2,1,0:T(8,128)}, f32[32,16,384]{2,1,0:T(8,128)}, u32[]{:S(2)}, u32[]{:S(2)}) collective-permute-start(f32[32,16,384]{2,1,0:T(8,128)} %get-tuple-element.214), channel_id=1, source_target_pairs={{0,2},{2,4},{4,6},{6,8},{8,10},{10,12},{12,14},{14,16},{16,18},{18... | collective-permute-start | bytes 2359304 | tf_op jit(solution)/shard_map/ppermute | solution.py:24
  232.8 24.0 %collective-permute-start.3 = (f32[32,16,384]{2,1,0:T(8,128)S(1)}, f32[32,16,384]{2,1,0:T(8,128)}, u32[]{:S(2)}, u32[]{:S(2)}) collective-permute-start(f32[32,16,384]{2,1,0:T(8,128)S(1)} %get-tuple-element.215), channel_id=1, source_target_pairs={{2,0},{4,2},{6,4},{8,6},{10,8},{12,10},{14,12},{16,14},{18,16},{20... | collective-permute-start | bytes 2359304 | tf_op jit(solution)/shard_map/ppermute | solution.py:25
  399.0 27.6 %all-to-all-start.5 = ((f32[2,16,16,1024]{3,2,1,0:T(8,128)}), f32[2,16,16,1024]{3,2,1,0:T(8,128)}, u32[]{:S(2)}, u32[]{:S(2)}) async-start(f32[2,16,16,1024]{3,2,1,0:T(8,128)} %pad_maximum_fusion.2), calls=%async_computation.5 | async-start | bytes 4194304 | tf_op jit(solution)/shard_map/all_to_all | solution.py:102
  406.2 25.1 %collective-permute-start.4 = (f32[32,16,384]{2,1,0:T(8,128)}, f32[32,16,384]{2,1,0:T(8,128)}, u32[]{:S(2)}, u32[]{:S(2)}) collective-permute-start(f32[32,16,384]{2,1,0:T(8,128)} %get-tuple-element.210), channel_id=1, source_target_pairs={{0,2},{2,4},{4,6},{6,8},{8,10},{10,12},{12,14},{14,16},{16,18},{18... | collective-permute-start | bytes 2359304 | tf_op jit(solution)/shard_map/ppermute | solution.py:24
  408.4 22.9 %collective-permute-start.5 = (f32[32,16,384]{2,1,0:T(8,128)S(1)}, f32[32,16,384]{2,1,0:T(8,128)}, u32[]{:S(2)}, u32[]{:S(2)}) collective-permute-start(f32[32,16,384]{2,1,0:T(8,128)S(1)} %get-tuple-element.211), channel_id=1, source_target_pairs={{2,0},{4,2},{6,4},{8,6},{10,8},{12,10},{14,12},{16,14},{18,16},{20... | collective-permute-start | bytes 2359304 | tf_op jit(solution)/shard_map/ppermute | solution.py:25
  576.7 27.5 %all-to-all-start.7 = ((f32[2,16,16,1024]{3,2,1,0:T(8,128)}), f32[2,16,16,1024]{3,2,1,0:T(8,128)}, u32[]{:S(2)}, u32[]{:S(2)}) async-start(f32[2,16,16,1024]{3,2,1,0:T(8,128)} %pad_maximum_fusion.3), calls=%async_computation.7 | async-start | bytes 4194304 | tf_op jit(solution)/shard_map/all_to_all | solution.py:102
  583.9 25.1 %collective-permute-start.6 = (f32[32,16,384]{2,1,0:T(8,128)}, f32[32,16,384]{2,1,0:T(8,128)}, u32[]{:S(2)}, u32[]{:S(2)}) collective-permute-start(f32[32,16,384]{2,1,0:T(8,128)} %get-tuple-element.206), channel_id=1, source_target_pairs={{0,2},{2,4},{4,6},{6,8},{8,10},{10,12},{12,14},{14,16},{16,18},{18... | collective-permute-start | bytes 2359304 | tf_op jit(solution)/shard_map/ppermute | solution.py:24
  586.1 22.9 %collective-permute-start.7 = (f32[32,16,384]{2,1,0:T(8,128)S(1)}, f32[32,16,384]{2,1,0:T(8,128)}, u32[]{:S(2)}, u32[]{:S(2)}) collective-permute-start(f32[32,16,384]{2,1,0:T(8,128)S(1)} %get-tuple-element.207), channel_id=1, source_target_pairs={{2,0},{4,2},{6,4},{8,6},{10,8},{12,10},{14,12},{16,14},{18,16},{20... | collective-permute-start | bytes 2359304 | tf_op jit(solution)/shard_map/ppermute | solution.py:25
  725.2 6.2 copy-start.35
  725.2 29.6 %all-to-all-start.8 = ((f32[32,16,1024]{2,1,0:T(8,128)}), f32[32,16,1024]{2,1,0:T(8,128)}, u32[]{:S(2)}, u32[]{:S(2)}) async-start(f32[32,16,1024]{2,1,0:T(8,128)} %copy.128), calls=%async_computation.8 | async-start | bytes 4194304 | tf_op jit(solution)/shard_map/all_to_all | solution.py:95
  763.0 28.2 %all-to-all-start.9 = ((f32[2,16,16,1024]{3,2,1,0:T(8,128)}), f32[2,16,16,1024]{3,2,1,0:T(8,128)}, u32[]{:S(2)}, u32[]{:S(2)}) async-start(f32[2,16,16,1024]{3,2,1,0:T(8,128)} %pad_maximum_fusion.4), calls=%async_computation.9 | async-start | bytes 4194304 | tf_op jit(solution)/shard_map/all_to_all | solution.py:102
  771.0 24.9 %collective-permute-start.8 = (f32[32,16,384]{2,1,0:T(8,128)}, f32[32,16,384]{2,1,0:T(8,128)}, u32[]{:S(2)}, u32[]{:S(2)}) collective-permute-start(f32[32,16,384]{2,1,0:T(8,128)} %get-tuple-element.202), channel_id=1, source_target_pairs={{0,2},{2,4},{4,6},{6,8},{8,10},{10,12},{12,14},{14,16},{16,18},{18... | collective-permute-start | bytes 2359304 | tf_op jit(solution)/shard_map/ppermute | solution.py:24
  773.2 22.8 %collective-permute-start.9 = (f32[32,16,384]{2,1,0:T(8,128)S(1)}, f32[32,16,384]{2,1,0:T(8,128)}, u32[]{:S(2)}, u32[]{:S(2)}) collective-permute-start(f32[32,16,384]{2,1,0:T(8,128)S(1)} %get-tuple-element.203), channel_id=1, source_target_pairs={{2,0},{4,2},{6,4},{8,6},{10,8},{12,10},{14,12},{16,14},{18,16},{20... | collective-permute-start | bytes 2359304 | tf_op jit(solution)/shard_map/ppermute | solution.py:25
  929.1 7.2 copy-start.6
  929.1 7.2 copy-start.12
  929.1 7.2 copy-start.14
  929.1 7.2 copy-start.27
  936.3 8.0 copy-start.1
  (22 other events, 75.3 us)
